TPU v7x, 32 devices: a whole 2x2x4 slice. The times are simulated.
32 devices in a mesh: sph: 32 (over z, y, x, core).
Axes of the slice: x: 2, y: 2, z: 4, core: 2. Of those that a mesh axis runs over, the one named last changes fastest.
Arguments:
- right_side: float32 [512, 2, 336], P('sph'), may hold values from -8 to 8
- positions: float32 [3, 512], P(None, 'sph'), may hold values from -0.1 to 15.1, as said below
- sphere_radii: float32 [512], P('sph'), may hold values from 0.2 to 0.35
- azimuths: float32 [512], P('sph'), may hold values from -3.1416 to 3.1416
- pair_flags: int32 [512, 512], P('sph'), may hold values from 0 to 2, as said below
- pair_counts: int32 [512], P('sph'), may hold values from 1 to 511, as said below
- tilt_matrix: float32 [336, 336], replicated, may hold values from -1 to 1
- axial_terms: float32 [8, 336, 336], replicated, may hold values from -1 to 1
Outputs:
- solution: float32 [512, 2, 336], P('sph')
- residual: float32 [512, 2, 336], P('sph')
- direction: float32 [512, 2, 336], P('sph')
Inputs may be any that keep to these rules, and one draw needn't show every extreme that they name: pair_flags is symmetric and zero on the diagonal. pair_counts[i] is the number of j with pair_flags[i, j] != 0; one sphere is linked to every other. `positions`: any two sphere centres are at least 0.8 apart.
All inputs are finite; a program needn't handle non-finite values.
Results may differ from a plain program's by a relative error of at most 0.0003.
Values sent between devices are 32-bit elements; how exact they have to be, the bound alone decides.
A program may use at most 64 MiB of HBM per device.

v0:
```python
import functools

import jax
import jax.numpy as jnp
import numpy as np
from jax import lax
from jax.experimental import pallas as pl
from jax.experimental.pallas import tpu as pltpu
from jax.sharding import PartitionSpec as P

coupling = 0.25
wavenum = 2.5
phase_step = 0.9
dist_floor = 0.8

LANES = 128
MESH = pl.DeviceIdType.MESH
BF = jnp.bfloat16
F32 = jnp.float32


def orders_table(half):
    degree, orders = 1, []
    while len(orders) < half:
        orders += list(range(-degree, degree + 1))
        degree += 1
    return np.asarray(orders, np.float32)


def split(value):
    high = value.astype(BF)
    return high, (value - high.astype(F32)).astype(BF)


def dot3(high, low, w_high, w_low):
    rows = high.shape[0]
    both = jnp.dot(
        jnp.concatenate([high, low], axis=0), w_high, preferred_element_type=F32
    )
    return (
        both[:rows]
        + both[rows:]
        + jnp.dot(high, w_low, preferred_element_type=F32)
    )


def kernel(
    n, S, C, CP, terms,
    r_ref, pos_ref, rad_ref, az_ref, counts_ref, flags_ref, orders_ref, tilt_ref, axial_ref,
    out_ref, rows_scr,
    own1, own2, buf1, buf2, f_hi, f_lo, w_hi, w_lo, t_hi, t_lo, tt_hi, tt_lo,
    g_raw, g_hi, g_lo, sums, g_sem, send_sem, recv_sem, sum_send, sum_recv,
):
    half = C // 2
    q = n // 8
    me = lax.axis_index("sph")
    core = lax.rem(me, 2)
    x_bit = lax.rem(me // 2, 2)
    y_bit = lax.rem(me // 4, 2)
    other = me + 1 - 2 * core
    x_nb = me + 2 - 4 * x_bit
    y_nb = me + 4 - 8 * y_bit
    near_a = x_nb * (1 - core) + y_nb * core
    near_b = y_nb * (1 - core) + x_nb * core
    diag = x_nb + y_nb - me

    z_at = me // 8

    def flipped(k):
        place, bit = z_at, 1
        while bit <= k:
            if k & bit:
                place = place + bit - 2 * bit * lax.rem(z_at // bit, 2)
            bit *= 2
        return place

    places = [flipped(k) for k in range(q)]
    if q == 4:
        low, high = lax.rem(z_at, 2), z_at // 2
        inner = low + high - 2 * low * high
        swing = inner * (places[3] - places[2])
        places[2], places[3] = places[2] + swing, places[3] - swing

    def shifted(base, k):
        return base + 8 * (places[k] - z_at)

    barrier = pltpu.get_barrier_semaphore()
    peers = [other, x_nb, y_nb, diag] + [shifted(me, k) for k in range(1, q)]
    for peer in peers:
        pl.semaphore_signal(barrier, inc=1, device_id=(peer,), device_id_type=MESH)
    axial_copy = pltpu.make_async_copy(axial_ref, g_raw, g_sem)
    axial_copy.start()

    rows_scr[...] = jnp.zeros_like(rows_scr)
    rows_scr[0:3, 0:S] = pos_ref[...]
    rows_scr[3:4, 0:S] = rad_ref[...]
    rows_scr[4:5, 0:S] = az_ref[...]
    rows_scr[5:6, 0:S] = counts_ref[...].astype(F32)
    cols = rows_scr[...].T[0:S]
    lane = lax.broadcasted_iota(jnp.int32, (S, CP), 1)
    phases = cols[:, 4:5] * orders_ref[...]
    cos_t = jnp.cos(phases)
    sin_t = jnp.sin(phases)
    cos2 = jnp.concatenate([cos_t, cos_t], axis=0)
    sin2 = jnp.concatenate([sin_t, sin_t], axis=0)
    lane2 = jnp.concatenate([lane, lane], axis=0)
    root = 1.0 / jnp.sqrt(1.0 + cols[:, 5:6])
    root2 = jnp.concatenate([root, root], axis=0)

    def swapped(v):
        return jnp.where(
            lane2 < half, -pltpu.roll(v, CP - half, 1), pltpu.roll(v, half, 1)
        )

    t_f32 = tilt_ref[...]
    th, tl = split(t_f32)
    for ref in (t_hi, t_lo, tt_hi, tt_lo):
        ref[...] = jnp.zeros_like(ref)
    t_hi[0:C, 0:C] = th
    t_lo[0:C, 0:C] = tl

    def framed(v):
        turned = cos2 * v + sin2 * swapped(v)
        high, low = split(turned)
        return dot3(high, low, t_hi[...], t_lo[...])

    pad = jnp.zeros((S, CP - C), F32)
    r_vec = jnp.concatenate(
        [
            jnp.concatenate([r_ref[:, 0, :], pad], axis=1),
            jnp.concatenate([r_ref[:, 1, :], pad], axis=1),
        ],
        axis=0,
    )

    def store_block(own, fr, extras):
        second = fr[S:]
        for i, extra in enumerate(extras):
            second = jnp.where(lane == C + i, extra, second)
        own[:, 0:CP] = fr[:S]
        own[:, CP:] = second

    def rows_of(origin):
        return pl.ds(pl.multiple_of(origin * S, S), S)

    def gather(phase, own, buf, fillers):
        sends = []

        def send(slot, k, src, origin, dev):
            copy = pltpu.make_async_remote_copy(
                src_ref=src,
                dst_ref=buf.at[rows_of(origin), :],
                send_sem=send_sem.at[phase, slot, k],
                recv_sem=recv_sem.at[phase, origin],
                device_id=(dev,),
                device_id_type=MESH,
            )
            copy.start()
            sends.append(copy)

        def absorb_value(x, origin):
            high, low = split(x)
            f_hi[rows_of(origin), :] = high
            f_lo[rows_of(origin), :] = low

        def arrive(origin):
            ref = buf.at[rows_of(origin), :]
            pltpu.make_async_remote_copy(
                src_ref=ref, dst_ref=ref,
                send_sem=send_sem.at[phase, 0, 0],
                recv_sem=recv_sem.at[phase, origin],
                device_id=(other,), device_id_type=MESH,
            ).wait_recv()
            return ref

        def absorb(origin):
            absorb_value(buf[rows_of(origin), :], origin)

        fillers = list(fillers)

        def fill():
            if fillers:
                fillers.pop(0)()

        relayed = ()

        def spread(k, ref, origin):
            send(2, k, ref, origin, near_b)
            send(1, k, ref, origin, near_a)
            if k not in relayed:
                send(3, k, ref, origin, diag)
            send(4, k, ref, origin, other)

        def take_a(k):
            origin = shifted(near_a, k)
            ref = arrive(origin)
            if k in relayed:
                send(3, k, ref, origin, near_b)
            send(5, k, ref, origin, other)
            absorb(origin)

        def take(slot, base, k):
            origin = shifted(base, k)
            ref = arrive(origin)
            send(slot, k, ref, origin, other)
            absorb(origin)

        for k in range(1, q):
            send(0, k, own, me, shifted(me, k))
        spread(0, own, me)
        mine = own[...]
        buf[rows_of(me), :] = mine
        absorb_value(mine, me)
        for _ in range(3):
            fill()
        for step in range(1, q + 2):
            if step < q:
                origin = shifted(me, step)
                spread(step, arrive(origin), origin)
                absorb(origin)
                fill()
            if step - 1 < q:
                take_a(step - 1)
                take(6, near_b, step - 1)
                fill()
            if 0 <= step - 2 < q:
                take(7, diag, step - 2)
                fill()
        while fillers:
            fill()
        flip = other - me
        for k in range(q):
            for base in (me, near_b, near_a, diag):
                origin = shifted(base, k) + flip
                arrive(origin)
                absorb(origin)
        return sends

    def apply_op():
        gathered = dot3(w_hi[...], w_lo[...], f_hi[...], f_lo[...])
        x = jnp.concatenate(
            [
                jnp.concatenate(
                    [gathered[m * S : (m + 1) * S, p * CP : (p + 1) * CP] for p in range(2)],
                    axis=0,
                )
                for m in range(terms)
            ],
            axis=1,
        )
        high, low = split(x)
        coupled = dot3(high, low, g_hi[...], g_lo[...])
        high, low = split(coupled)
        unturned = dot3(high, low, tt_hi[...], tt_lo[...]) * root2
        return cos2 * unturned - sin2 * swapped(unturned)

    store_block(own1, framed(r_vec), [cols[:, i : i + 1] for i in range(4)])
    pl.semaphore_wait(barrier, len(peers))

    def fill_tilt():
        h2, l2 = split(t_f32.T)
        tt_hi[0:C, 0:C] = h2
        tt_lo[0:C, 0:C] = l2

    def fill_zero():
        g_hi[...] = jnp.zeros_like(g_hi)
        g_lo[...] = jnp.zeros_like(g_lo)
        axial_copy.wait()

    def fill_axial(m):
        h2, l2 = split(g_raw[m])
        g_hi[m * CP : m * CP + C, 0:C] = h2
        g_lo[m * CP : m * CP + C, 0:C] = l2

    fillers = [fill_tilt, fill_zero] + [
        functools.partial(fill_axial, m) for m in range(terms)
    ]
    sends = gather(0, own1, buf1, fillers)

    geo = buf1[:, 2 * CP - LANES :].T
    at = C - (CP - LANES)
    dx = cols[:, 0:1] - geo[at : at + 1]
    dy = cols[:, 1:2] - geo[at + 1 : at + 2]
    dz = cols[:, 2:3] - geo[at + 2 : at + 3]
    distance = jnp.sqrt(dx * dx + dy * dy + dz * dz)
    ratio = (cols[:, 3:4] + geo[at + 3 : at + 4]) / jnp.maximum(distance, dist_floor)
    flags = flags_ref[...]
    wave = wavenum * distance
    cos_w = coupling * jnp.cos(wave)
    sin_w = coupling * jnp.sin(wave)
    power = jnp.ones_like(distance)
    for m in range(terms):
        turn_c = float(np.cos(phase_step * m))
        turn_s = float(np.sin(phase_step * m))
        keep = (flags != 0) if m == 0 else (flags == 1)
        weight = jnp.where(keep, power * (turn_c * cos_w - turn_s * sin_w), 0.0)
        power = power * ratio
        high, low = split(weight)
        w_hi[m * S : (m + 1) * S, :] = high
        w_lo[m * S : (m + 1) * S, :] = low

    p_vec = r_vec - apply_op()

    def per_sphere(a, b):
        both = jnp.sum(a * b, axis=1, keepdims=True)
        return both[:S] + both[S:]

    store_block(own2, framed(p_vec), [per_sphere(r_vec, r_vec), per_sphere(r_vec, p_vec)])
    sends += gather(1, own2, buf2, [])
    q_vec = p_vec - apply_op()

    starts = jnp.sum(buf2[:, 2 * CP - LANES :], axis=0, keepdims=True)
    rho_start = starts[:, at : at + 1]
    alpha = rho_start / starts[:, at + 1 : at + 2]
    half_step = r_vec - alpha * p_vec
    half_image = p_vec - alpha * q_vec

    def total(a, b):
        return jnp.sum(jnp.sum(a * b, axis=0, keepdims=True), axis=1, keepdims=True)

    lane1 = lax.broadcasted_iota(jnp.int32, (1, LANES), 1)
    row = jnp.zeros((1, LANES), F32)
    pairs = (
        (half_image, half_step),
        (half_image, half_image),
        (r_vec, half_step),
        (r_vec, half_image),
    )
    for i, (a, b) in enumerate(pairs):
        row = jnp.where(lane1 == i, total(a, b), row)
    sums[me] = row

    def sum_copy(k, origin, dev):
        return pltpu.make_async_remote_copy(
            src_ref=sums.at[origin],
            dst_ref=sums.at[origin],
            send_sem=sum_send.at[k],
            recv_sem=sum_recv.at[origin],
            device_id=(dev,),
            device_id_type=MESH,
        )

    @pl.loop(1, n)
    def _(k):
        sum_copy(k, me, lax.rem(me + k, n)).start()

    for copy in sends:
        copy.wait_send()

    @pl.loop(1, n)
    def _(k):
        peer = lax.rem(me + k, n)
        sum_copy(k, peer, peer).wait_recv()

    all_sums = jnp.sum(sums[...], axis=0)
    t_s, t_t, r_s, r_t = [all_sums[:, i : i + 1] for i in range(4)]
    omega = t_s / t_t
    rho_next = r_s - omega * r_t
    beta = rho_next / rho_start * (alpha / omega)
    sol = alpha * r_vec + omega * half_step
    res = half_step - omega * half_image
    direction = res + beta * (r_vec - omega * p_vec)
    for i, val in enumerate((sol, res, direction)):
        for p in range(2):
            out_ref[i, :, p, :] = val[p * S : (p + 1) * S, 0:C]

    @pl.loop(1, n)
    def _(k):
        sum_copy(k, me, lax.rem(me + k, n)).wait_send()


def solution(mesh):
    n = mesh.shape["sph"]

    def on_device(
        right_side, positions, sphere_radii, azimuths, pair_flags, pair_counts, tilt_matrix, axial_terms
    ):
        S, _, C = right_side.shape
        CP = -(-C // LANES) * LANES
        terms = axial_terms.shape[0]
        total = pair_flags.shape[1]
        q = n // 8
        table = orders_table(C // 2)
        orders = np.zeros((1, CP), np.float32)
        orders[0, : C // 2] = table
        orders[0, C // 2 : C] = table
        vmem = pl.BlockSpec(memory_space=pltpu.VMEM)
        out = pltpu.VMEM((3,) + right_side.shape, F32)
        stacked = pl.pallas_call(
            functools.partial(kernel, n, S, C, CP, terms),
            out_shape=out,
            in_specs=[vmem] * 8 + [pl.BlockSpec(memory_space=pl.ANY)],
            out_specs=vmem,
            scratch_shapes=[
                pltpu.VMEM((8, LANES), F32),
                pltpu.VMEM((S, 2 * CP), F32),
                pltpu.VMEM((S, 2 * CP), F32),
                pltpu.VMEM((total, 2 * CP), F32),
                pltpu.VMEM((total, 2 * CP), F32),
                pltpu.VMEM((total, 2 * CP), BF),
                pltpu.VMEM((total, 2 * CP), BF),
                pltpu.VMEM((terms * S, total), BF),
                pltpu.VMEM((terms * S, total), BF),
                pltpu.VMEM((CP, CP), BF),
                pltpu.VMEM((CP, CP), BF),
                pltpu.VMEM((CP, CP), BF),
                pltpu.VMEM((CP, CP), BF),
                pltpu.VMEM((terms, C, C), F32),
                pltpu.VMEM((terms * CP, CP), BF),
                pltpu.VMEM((terms * CP, CP), BF),
                pltpu.VMEM((n, 1, LANES), F32),
                pltpu.SemaphoreType.DMA,
                pltpu.SemaphoreType.DMA((2, 8, q)),
                pltpu.SemaphoreType.DMA((2, n)),
                pltpu.SemaphoreType.DMA((n,)),
                pltpu.SemaphoreType.DMA((n,)),
            ],
            compiler_params=pltpu.CompilerParams(
                collective_id=0, has_side_effects=True, vmem_limit_bytes=60 * 1024 * 1024
            ),
        )(
            right_side,
            positions,
            sphere_radii.reshape(1, S),
            azimuths.reshape(1, S),
            pair_counts.reshape(1, S),
            pair_flags,
            jnp.asarray(orders),
            tilt_matrix,
            axial_terms,
        )
        return (stacked[0], stacked[1], stacked[2])

    in_specs = (
        P("sph", None, None),
        P(None, "sph"),
        P("sph"),
        P("sph"),
        P("sph", None),
        P("sph"),
        P(),
        P(),
    )
    out_specs = (P("sph", None, None), P("sph", None, None), P("sph", None, None))
    return jax.shard_map(
        on_device, mesh=mesh, in_specs=in_specs, out_specs=out_specs, check_vma=False
    )
```

profile of v0, /device:TPU:0, one launch (start us, length us, event | category | flops | bytes accessed | tf_op | source)
XLA Modules:
  0.0 45.1 jit_solution(5771383141819100793)
XLA Ops:
  0.6 43.7 %shard_map.112 = f32[3,16,2,336]{3,2,1,0:T(2,128)S(1)} custom-call(f32[16,2,336]{2,1,0:T(2,128)} %r_ref.1, f32[3,16]{1,0:T(4,128)} %pos_ref.1, f32[1,16]{1,0:T(1,128)} %bitcast.9, f32[1,16]{1,0:T(1,128)} %bitcast.10, s32[1,16]{1,0:T(1,128)} %bitcast.11, s32[16,512]{1,0:T(8,128)} %flags_ref.1, f32[1,384]{1,0:T(1,128)} %constant.2.clone.orders_ref, ...), custom_call_target="tpu_custom_call" | custom-call | tf_op jit(solution)/shard_map/pallas_call | solution.py:389
  44.4 0.7 %slice_bitcast_fusion = (f32[16,2,336]{2,1,0:T(2,128)}, f32[16,2,336]{2,1,0:T(2,128)}, f32[16,2,336]{2,1,0:T(2,128)}) fusion(f32[3,16,2,336]{3,2,1,0:T(2,128)S(1)} %shard_map.112), kind=kLoop, calls=%fused_computation | loop fusion | bytes 258048 | tf_op jit(solution)/shard_map/squeeze | solution.py:432
where the time goes:
time: 45.2 us; the launch traced here: 45.1 us
  Pallas kernels  43.7 us (97%)
  local copies, waits for them, and re-layouts  0.67 us (1%)
  between operations  0.64 us (1%)
    pallas_call x1, Pallas kernels, on_device(): pl.pallas_call(functools.partial(kernel, n, S, C, CP, terms), out_shape=o...  43.7 us

commit v1 on v0

v1 whole, which is shorter than its diff:
```python
import functools

import jax
import jax.numpy as jnp
import numpy as np
from jax import lax
from jax.experimental import pallas as pl
from jax.experimental.pallas import tpu as pltpu
from jax.sharding import PartitionSpec as P

coupling = 0.25
wavenum = 2.5
phase_step = 0.9
dist_floor = 0.8

LANES = 128
MESH = pl.DeviceIdType.MESH
BF = jnp.bfloat16
F32 = jnp.float32

TREES = (
    (0, 0, 0, 0, 0, 4, 2, 3, 4, 8, 8, 3, 0, 12, 2, 12),
    (4, 0, 0, 0, 4, 4, 4, 4, 4, 8, 8, 10, 8, 9, 12, 7),
)
RANKS = (
    (5, 2, 5, 8, 6, 11, 4, 9, 11, 3, 4, 4, 8, 15, 13, 6),
    (8, 10, 2, 4, 12, 3, 1, 8, 2, 11, 0, 7, 7, 13, 7, 0),
)
ORDERS = (
    (1, 2, 4, 3, 12, 8, 6, 5, 7, 14, 10, 13, 9, 11, 15),
    (0, 5, 6, 8, 7, 2, 10, 12, 1, 9, 14, 11, 13, 15, 3),
)


def children(kind, node):
    found = [i for i in range(16) if i != 4 * kind and TREES[kind][i] == node]
    return sorted(found, key=lambda i: RANKS[kind][i])


def route(q):
    if q != 4:
        firsts = [(1, 0), (2, 0), (3, 0)] + [(0, k) for k in range(1, q)]
        takes = []
        for k in range(q):
            if k + 1 < q:
                takes.append(((0, k + 1), [(1, k + 1), (2, k + 1), (3, k + 1)]))
            takes += [((ab, k), []) for ab in (1, 2, 3)]
        return [(firsts, takes)]
    kinds = []
    for own in range(2):
        firsts = [(k % 4, k // 4) for k in children(own, 4 * own)]
        takes = []
        for source in ORDERS[own]:
            ab, z = source % 4, source // 4
            kind = min(z, 3 - z)
            node = ab + 4 * (own if z < 2 else 3 - own)
            nexts = [
                ((k % 4) ^ ab, k // 4 if z < 2 else 3 - k // 4)
                for k in children(kind, node)
            ]
            takes.append(((ab, z), nexts))
        kinds.append((firsts, takes))
    return kinds


def orders_table(half):
    degree, orders = 1, []
    while len(orders) < half:
        orders += list(range(-degree, degree + 1))
        degree += 1
    return np.asarray(orders, np.float32)


def split(value):
    high = value.astype(BF)
    return high, (value - high.astype(F32)).astype(BF)


def dot3(high, low, w_high, w_low):
    rows = high.shape[0]
    both = jnp.dot(
        jnp.concatenate([high, low], axis=0), w_high, preferred_element_type=F32
    )
    return (
        both[:rows]
        + both[rows:]
        + jnp.dot(high, w_low, preferred_element_type=F32)
    )


def kernel(
    n, S, C, CP, terms,
    r_ref, pos_ref, rad_ref, az_ref, counts_ref, flags_ref, orders_ref, tilt_ref, axial_ref,
    out_ref,
    r_v, t_raw, flags_v, rows_own, rows_oth, r_own, r_oth,
    own1, own2, buf1, buf2, f_hi, f_lo, w_all, acc,
    t_hi, t_lo, tt_hi, tt_lo, gg_hi, gg_lo, g_raw, g_hi, g_lo,
    p_scr, q_scr, p_fin, q_fin, part_own, part_oth, s3, t3, p3, sums,
    in_sem, send_sem, recv_sem, pair_send, pair_recv, sum_send, sum_recv,
):
    half = C // 2
    q = n // 8
    S2 = 2 * S
    PL = 8 * S
    kinds = route(q)
    me = lax.axis_index("sph")
    core = lax.rem(me, 2)
    x_bit = lax.rem(me // 2, 2)
    y_bit = lax.rem(me // 4, 2)
    z_at = me // 8
    chip = me - core
    other = chip + 1 - core
    chip_x = chip + 2 - 4 * x_bit
    chip_y = chip + 4 - 8 * y_bit
    chip_d = chip_x + chip_y - chip

    if q == 4:
        mirror = z_at // 2
        at_end = (z_at + mirror * (3 - 2 * z_at)) == 0
        conds = [at_end, jnp.logical_not(at_end)]

        def place(k):
            return k + mirror * (3 - 2 * k)
    else:
        conds = [None]

        def place(k):
            at, bit = z_at, 1
            while bit <= k:
                if k & bit:
                    at = at + bit - 2 * bit * lax.rem(z_at // bit, 2)
                bit *= 2
            return at

    def pick(values):
        if len(values) == 1:
            return values[0]
        return jnp.where(at_end, values[0], values[1])

    def guarded(index, body):
        if conds[index] is None:
            body()
        else:
            pl.when(conds[index])(body)

    chip_a = chip_x * (1 - core) + chip_y * core
    chip_b = chip_y * (1 - core) + chip_x * core
    own_bases = (chip, chip_a, chip_b, chip_d)
    pol_bases = ((chip, chip_x, chip_y, chip_d), (chip, chip_y, chip_x, chip_d))

    def chip_at(bases, where):
        return bases[where[0]] + 8 * (place(where[1]) - z_at)

    barrier = pltpu.get_barrier_semaphore()
    line = [chip_at(own_bases, (0, k)) for k in range(q)] if q != 4 else None
    if q == 4:
        line = [chip + 8 * (lax.rem(z_at + k, q) - z_at) for k in range(1, q)]
    else:
        line = line[1:]
    peers = [other]
    for base in [chip_x, chip_y, chip_d] + line:
        peers += [base, base + 1]
    for peer in peers:
        pl.semaphore_signal(barrier, inc=1, device_id=(peer,), device_id_type=MESH)

    core_rows = pl.ds(pl.multiple_of(core * S, S), S)
    other_rows = pl.ds(pl.multiple_of((1 - core) * S, S), S)
    r_copy = pltpu.make_async_copy(r_ref, r_v, in_sem.at[0])
    t_copy = pltpu.make_async_copy(tilt_ref, t_raw, in_sem.at[1])
    f_copy = pltpu.make_async_copy(flags_ref, flags_v.at[core_rows, :], in_sem.at[2])
    g_copy = pltpu.make_async_copy(axial_ref, g_raw, in_sem.at[3])
    for copy in (r_copy, t_copy, f_copy, g_copy):
        copy.start()

    rows_own[...] = jnp.zeros_like(rows_own)
    rows_own[0:3, 0:S] = pos_ref[...]
    rows_own[3:4, 0:S] = rad_ref[...]
    rows_own[4:5, 0:S] = az_ref[...]
    rows_own[5:6, 0:S] = counts_ref[...].astype(F32)
    cols = rows_own[...].T[0:S]
    lane = lax.broadcasted_iota(jnp.int32, (S, CP), 1)
    lane2 = lax.broadcasted_iota(jnp.int32, (S2, CP), 1)

    def swapped(v):
        return jnp.where(
            lane2 < half, -pltpu.roll(v, CP - half, 1), pltpu.roll(v, half, 1)
        )

    def padded(v):
        return jnp.concatenate([v, jnp.zeros((v.shape[0], CP - C), v.dtype)], axis=1)

    phases = cols[:, 4:5] * orders_ref[...]
    cos_o = jnp.cos(phases)
    sin_o = jnp.sin(phases)
    cos2 = jnp.concatenate([cos_o, cos_o], axis=0)
    sin2 = jnp.concatenate([sin_o, sin_o], axis=0)

    t_copy.wait()
    for ref in (t_hi, t_lo):
        ref[C:CP, :] = jnp.zeros((CP - C, CP), BF)
    th, tl = split(t_raw[...])
    t_hi[0:C, :] = padded(th)
    t_lo[0:C, :] = padded(tl)
    r_copy.wait()
    for p in range(2):
        r_own[p] = padded(r_v[:, p, :])
    r_vec = jnp.concatenate([r_own[0], r_own[1]], axis=0)
    turned = cos2 * r_vec + sin2 * swapped(r_vec)
    high, low = split(turned)
    framed = dot3(high, low, t_hi[...], t_lo[...])
    for p in range(2):
        block = framed[p * S : (p + 1) * S]
        for i in range(4):
            block = jnp.where(lane == C + i, cols[:, i : i + 1], block)
        own1[p] = block

    def chip_rows(origin):
        return pl.ds(pl.multiple_of(origin * S, S2), S2)

    def dev_rows(origin):
        return pl.ds(pl.multiple_of(origin * S, S), S)

    buf1[dev_rows(me), :] = own1[core]

    waits = [[] for _ in conds]
    loose = []

    def remote(src, dst, s_sem, r_sem, dev):
        return pltpu.make_async_remote_copy(
            src_ref=src, dst_ref=dst, send_sem=s_sem, recv_sem=r_sem,
            device_id=(dev,), device_id_type=MESH,
        )

    def pair_copy(i, src, dst):
        return remote(src, dst, pair_send.at[i], pair_recv.at[i], other)

    def pair_start(i, src, dst):
        copy = pair_copy(i, src, dst)
        copy.start()
        loose.append(copy)

    counters = {}

    def next_sem(phase, kind):
        i = counters.get((phase, kind), 0)
        counters[(phase, kind)] = i + 1
        return send_sem.at[phase, i]

    def dispatch(kind, copies):
        if not copies:
            return
        waits[kind].extend(copies)

        def body():
            for copy in copies:
                copy.start()

        guarded(kind, body)

    def first_sends(phase, buf):
        for kind, (firsts, _) in enumerate(kinds):
            copies = []
            for where in firsts:
                if phase == 0:
                    for p in range(2):
                        copies.append(
                            remote(
                                own1.at[p], buf.at[dev_rows(me), :],
                                next_sem(phase, kind), recv_sem.at[phase, chip // 2],
                                chip_at(pol_bases[p], where) + p,
                            )
                        )
                else:
                    copies.append(
                        remote(
                            own2, buf.at[chip_rows(chip), :],
                            next_sem(phase, kind), recv_sem.at[phase, chip // 2],
                            chip_at(own_bases, where) + core,
                        )
                    )
            dispatch(kind, copies)

    seen = []
    for firsts, takes in kinds:
        counts = {}
        done = []
        own_z = 0 if q != 4 else len(seen)
        counts[own_z] = 1
        for i, ((ab, z), _) in enumerate(takes):
            counts[z] = counts.get(z, 0) + 1
            if counts[z] == 4:
                done.append((z, i))
        seen.append(done)
    slot_of = [{z: s for s, (z, _) in enumerate(done)} for done in seen]
    ready = [max(done[s][1] for done in seen) for s in range(q)]

    def absorb(buf, origin, slot):
        at = pl.ds(pl.multiple_of(slot * PL + lax.rem(origin, 8) * S, S2), S2)
        high, low = split(buf[chip_rows(origin), :])
        f_hi[at, :] = high
        f_lo[at, :] = low

    def plane(slot):
        return pick([place(done[slot][0]) for done in seen])

    def gather_product(pair):
        k0 = 2 * PL * pair
        ks = slice(k0, k0 + 2 * PL)
        rows = terms * S2
        both = jnp.dot(w_all[:, ks], f_hi[ks, :], preferred_element_type=F32)
        total = (
            both[:rows]
            + both[rows:]
            + jnp.dot(w_all[0:rows, ks], f_lo[ks, :], preferred_element_type=F32)
        )
        if pair > 0:
            total = total + acc[...]
        if pair < q // 2 - 1:
            acc[...] = total
        return total

    def gather(phase, buf, fillers, on_plane):
        fillers = list(fillers)
        steps = len(kinds[0][1])
        gathered = None
        for i in range(steps):
            origin = pick([chip_at(own_bases, takes[i][0]) for _, takes in kinds])
            slot = pick([slot_of[j][takes[i][0][1]] for j, (_, takes) in enumerate(kinds)])
            ref = buf.at[chip_rows(origin), :]
            remote(
                ref, ref, send_sem.at[phase, 0], recv_sem.at[phase, origin // 2], other
            ).wait_recv()
            for kind, (_, takes) in enumerate(kinds):
                dispatch(
                    kind,
                    [
                        remote(
                            ref, ref, next_sem(phase, kind),
                            recv_sem.at[phase, origin // 2],
                            chip_at(own_bases, where) + core,
                        )
                        for where in takes[i][1]
                    ],
                )
            absorb(buf, origin, slot)
            if fillers:
                fillers.pop(0)()
            for s in range(q):
                if ready[s] == i:
                    if s == 0:
                        while fillers:
                            fillers.pop(0)()
                    on_plane(s)
                    if s % 2 == 1:
                        gathered = gather_product(s // 2)
        return gathered

    pl.semaphore_wait(barrier, len(peers))
    first_sends(0, buf1)
    pair_start(0, own1.at[1 - core], buf1.at[dev_rows(me), :])
    pair_start(1, rows_own, rows_oth)
    pair_start(2, r_own.at[1 - core], r_oth)
    f_copy.wait()
    pair_start(3, flags_v.at[core_rows, :], flags_v.at[core_rows, :])

    def pair_wait(i, ref):
        pair_copy(i, ref, ref).wait_recv()

    zeros_pad = jnp.zeros((CP - C, CP), BF)

    def fill_tilt():
        h2, l2 = split(t_raw[...].T)
        for ref, v in ((tt_hi, h2), (tt_lo, l2)):
            ref[0:C, :] = padded(v)
            ref[C:CP, :] = zeros_pad

    def fill_gram():
        h2, l2 = split(dot3(tt_hi[...], tt_lo[...], t_hi[...], t_lo[...]))
        gg_hi[...] = h2
        gg_lo[...] = l2

    def fill_axial(m):
        h2, l2 = split(g_raw[m])
        for ref, v in ((g_hi, h2), (g_lo, l2)):
            ref[m * CP : m * CP + C, :] = padded(v)
            ref[m * CP + C : (m + 1) * CP, :] = zeros_pad

    fill_tilt()
    g_copy.wait()
    pair_wait(1, rows_oth)
    cols_oth = rows_oth[...].T[0:S]
    first = core == 0
    cols2 = jnp.concatenate(
        [jnp.where(first, cols, cols_oth), jnp.where(first, cols_oth, cols)], axis=0
    )
    phases = cols2[:, 4:5] * orders_ref[...]
    cos_t = jnp.cos(phases)
    sin_t = jnp.sin(phases)
    root = 1.0 / jnp.sqrt(1.0 + cols2[:, 5:6])
    pair_wait(2, r_oth)
    r_mine = r_own[core]
    r32 = jnp.concatenate(
        [jnp.where(first, r_mine, r_oth[...]), jnp.where(first, r_oth[...], r_mine)], axis=0
    )
    pair_wait(3, flags_v.at[other_rows, :])
    pair_wait(0, buf1.at[dev_rows(other), :])
    own_slot = pick([slot_of[j][0 if q != 4 else j] for j in range(len(kinds))])
    absorb(buf1, chip, own_slot)

    at = C - (CP - LANES)

    def weights(s):
        z = plane(s)
        geo = buf1[pl.ds(pl.multiple_of(z * PL, PL), PL), CP - LANES :].T
        flags = flags_v[:, pl.ds(pl.multiple_of(z * PL, PL), PL)]
        dx = cols2[:, 0:1] - geo[at : at + 1]
        dy = cols2[:, 1:2] - geo[at + 1 : at + 2]
        dz = cols2[:, 2:3] - geo[at + 2 : at + 3]
        distance = jnp.sqrt(dx * dx + dy * dy + dz * dz)
        ratio = (cols2[:, 3:4] + geo[at + 3 : at + 4]) / jnp.maximum(distance, dist_floor)
        wave = wavenum * distance
        cos_w = coupling * jnp.cos(wave)
        sin_w = coupling * jnp.sin(wave)
        power = jnp.ones_like(distance)
        for m in range(terms):
            turn_c = float(np.cos(phase_step * m))
            turn_s = float(np.sin(phase_step * m))
            keep = (flags != 0) if m == 0 else (flags == 1)
            weight = jnp.where(keep, power * (turn_c * cos_w - turn_s * sin_w), 0.0)
            power = power * ratio
            high, low = split(weight)
            w_all[m * S2 : (m + 1) * S2, s * PL : (s + 1) * PL] = high
            w_all[(terms + m) * S2 : (terms + m + 1) * S2, s * PL : (s + 1) * PL] = low

    def couple(gathered):
        x = jnp.concatenate(
            [gathered[m * S2 : (m + 1) * S2] for m in range(terms)], axis=1
        )
        high, low = split(x)
        return dot3(high, low, g_hi[...], g_lo[...])

    def unframed(coupled):
        high, low = split(coupled)
        v = dot3(high, low, tt_hi[...], tt_lo[...]) * root
        return cos_t * v - sin_t * swapped(v)

    fillers = [functools.partial(fill_axial, m) for m in range(terms)] + [fill_gram]
    coupled = couple(gather(0, buf1, fillers, weights))

    framed = buf1[chip_rows(chip), :]
    high, low = split(coupled)
    block = framed - dot3(high, low, gg_hi[...], gg_lo[...]) * root
    r_r = jnp.sum(r32 * r32, axis=1, keepdims=True)
    r_p = r_r - root * jnp.sum(framed * coupled, axis=1, keepdims=True)
    block = jnp.where(lane2 == C, r_r, block)
    block = jnp.where(lane2 == C + 1, r_p, block)
    own2[...] = block
    first_sends(1, buf2)
    buf2[chip_rows(chip), :] = block
    absorb(buf2, chip, own_slot)

    p_vec = r32 - unframed(coupled)
    p_scr[...] = p_vec
    pair_start(4, p_scr.at[other_rows, :], p_fin.at[core])
    p_fin[core] = p_scr[core_rows, :]

    gathered = gather(1, buf2, [], lambda s: None)
    part_own[...] = jnp.broadcast_to(
        jnp.sum(buf2[:, CP - LANES :], axis=0, keepdims=True), part_own.shape
    )
    pair_start(5, part_own, part_oth)
    q_vec = p_vec - unframed(couple(gathered))
    q_scr[...] = q_vec
    pair_start(6, q_scr.at[other_rows, :], q_fin.at[core])
    q_fin[core] = q_scr[core_rows, :]

    pair_wait(5, part_oth)
    starts = part_own[0:1] + part_oth[0:1]
    rho_start = starts[:, at : at + 1]
    alpha = rho_start / starts[:, at + 1 : at + 2]
    half_step = r32 - alpha * p_vec
    half_image = p_vec - alpha * q_vec

    def total(a, b):
        return jnp.sum(jnp.sum(a * b, axis=0, keepdims=True), axis=1, keepdims=True)

    lane1 = lax.broadcasted_iota(jnp.int32, (1, LANES), 1)
    row = jnp.zeros((1, LANES), F32)
    pairs = (
        (half_image, half_step),
        (half_image, half_image),
        (r32, half_step),
        (r32, half_image),
    )
    for i, (a, b) in enumerate(pairs):
        row = jnp.where(lane1 == i, total(a, b), row)
    sums[me] = row

    def sum_copy(k, origin, dev):
        return remote(
            sums.at[origin], sums.at[origin], sum_send.at[k], sum_recv.at[origin], dev
        )

    @pl.loop(1, n)
    def _(k):
        sum_copy(k, me, lax.rem(me + k, n)).start()

    pair_wait(4, p_fin.at[1 - core])
    pair_wait(6, q_fin.at[1 - core])
    for p in range(2):
        p_p = p_fin[p]
        s3[:, p, :] = (r_own[p] - alpha * p_p)[:, 0:C]
        t3[:, p, :] = (p_p - alpha * q_fin[p])[:, 0:C]
        p3[:, p, :] = p_p[:, 0:C]

    for copy in loose:
        copy.wait_send()
    for kind, copies in enumerate(waits):

        def body(copies=copies):
            for copy in copies:
                copy.wait_send()

        guarded(kind, body)

    @pl.loop(1, n)
    def _(k):
        peer = lax.rem(me + k, n)
        sum_copy(k, peer, peer).wait_recv()

    all_sums = jnp.sum(sums[...], axis=0)
    t_s, t_t, r_s, r_t = [all_sums[:, i : i + 1] for i in range(4)]
    omega = t_s / t_t
    rho_next = r_s - omega * r_t
    beta = rho_next / rho_start * (alpha / omega)
    alpha = alpha.reshape(1, 1, 1)
    omega = omega.reshape(1, 1, 1)
    beta = beta.reshape(1, 1, 1)
    r_val = r_v[...]
    s_val = s3[...]
    res = s_val - omega * t3[...]
    out_ref[0] = alpha * r_val + omega * s_val
    out_ref[1] = res
    out_ref[2] = res + beta * (r_val - omega * p3[...])

    @pl.loop(1, n)
    def _(k):
        sum_copy(k, me, lax.rem(me + k, n)).wait_send()


def solution(mesh):
    n = mesh.shape["sph"]

    def on_device(
        right_side, positions, sphere_radii, azimuths, pair_flags, pair_counts, tilt_matrix, axial_terms
    ):
        S, _, C = right_side.shape
        CP = -(-C // LANES) * LANES
        terms = axial_terms.shape[0]
        total = pair_flags.shape[1]
        q = n // 8
        most = max(
            2 * len(firsts) + sum(len(nexts) for _, nexts in takes)
            for firsts, takes in route(q)
        )
        table = orders_table(C // 2)
        orders = np.zeros((1, CP), np.float32)
        orders[0, : C // 2] = table
        orders[0, C // 2 : C] = table
        vmem = pl.BlockSpec(memory_space=pltpu.VMEM)
        anywhere = pl.BlockSpec(memory_space=pl.ANY)
        out = pltpu.VMEM((3,) + right_side.shape, F32)
        stacked = pl.pallas_call(
            functools.partial(kernel, n, S, C, CP, terms),
            out_shape=out,
            in_specs=[anywhere, vmem, vmem, vmem, vmem, anywhere, vmem, anywhere, anywhere],
            out_specs=vmem,
            scratch_shapes=[
                pltpu.VMEM((S, 2, C), F32),
                pltpu.VMEM((C, C), F32),
                pltpu.VMEM((2 * S, total), jnp.int32),
                pltpu.VMEM((8, LANES), F32),
                pltpu.VMEM((8, LANES), F32),
                pltpu.VMEM((2, S, CP), F32),
                pltpu.VMEM((S, CP), F32),
                pltpu.VMEM((2, S, CP), F32),
                pltpu.VMEM((2 * S, CP), F32),
                pltpu.VMEM((total, CP), F32),
                pltpu.VMEM((total, CP), F32),
                pltpu.VMEM((total, CP), BF),
                pltpu.VMEM((total, CP), BF),
                pltpu.VMEM((4 * terms * S, total), BF),
                pltpu.VMEM((2 * terms * S, CP), F32),
                pltpu.VMEM((CP, CP), BF),
                pltpu.VMEM((CP, CP), BF),
                pltpu.VMEM((CP, CP), BF),
                pltpu.VMEM((CP, CP), BF),
                pltpu.VMEM((CP, CP), BF),
                pltpu.VMEM((CP, CP), BF),
                pltpu.VMEM((terms, C, C), F32),
                pltpu.VMEM((terms * CP, CP), BF),
                pltpu.VMEM((terms * CP, CP), BF),
                pltpu.VMEM((2 * S, CP), F32),
                pltpu.VMEM((2 * S, CP), F32),
                pltpu.VMEM((2, S, CP), F32),
                pltpu.VMEM((2, S, CP), F32),
                pltpu.VMEM((8, LANES), F32),
                pltpu.VMEM((8, LANES), F32),
                pltpu.VMEM((S, 2, C), F32),
                pltpu.VMEM((S, 2, C), F32),
                pltpu.VMEM((S, 2, C), F32),
                pltpu.VMEM((n, 1, LANES), F32),
                pltpu.SemaphoreType.DMA((4,)),
                pltpu.SemaphoreType.DMA((2, most)),
                pltpu.SemaphoreType.DMA((2, n // 2)),
                pltpu.SemaphoreType.DMA((7,)),
                pltpu.SemaphoreType.DMA((7,)),
                pltpu.SemaphoreType.DMA((n,)),
                pltpu.SemaphoreType.DMA((n,)),
            ],
            compiler_params=pltpu.CompilerParams(
                collective_id=0, has_side_effects=True, vmem_limit_bytes=60 * 1024 * 1024
            ),
        )(
            right_side,
            positions,
            sphere_radii.reshape(1, S),
            azimuths.reshape(1, S),
            pair_counts.reshape(1, S),
            pair_flags,
            jnp.asarray(orders),
            tilt_matrix,
            axial_terms,
        )
        return (stacked[0], stacked[1], stacked[2])

    in_specs = (
        P("sph", None, None),
        P(None, "sph"),
        P("sph"),
        P("sph"),
        P("sph", None),
        P("sph"),
        P(),
        P(),
    )
    out_specs = (P("sph", None, None), P("sph", None, None), P("sph", None, None))
    return jax.shard_map(
        on_device, mesh=mesh, in_specs=in_specs, out_specs=out_specs, check_vma=False
    )
```

time: 45.2 us -> 41.5 us (0.918)
  Pallas kernels: 43.7 us -> 40.1 us
    pallas_call x1, Pallas kernels: 43.7 us -> 40.1 us  [on_device(): pl.pallas_call(functools.partial(kernel, n, S, C, CP, terms), out_shape=o...]
where the time goes in v1:
time: 41.5 us; the launch traced here: 41.4 us
  Pallas kernels  40.1 us (97%)
  local copies, waits for them, and re-layouts  0.67 us (2%)
  between operations  0.64 us (2%)
    pallas_call x1, Pallas kernels, on_device(): pl.pallas_call(functools.partial(kernel, n, S, C, CP, terms), out_shape=o...  40.1 us

profile of v1, /device:TPU:0, one launch (start us, length us, event | category | flops | bytes accessed | tf_op | source)
XLA Modules:
  0.0 41.4 jit_solution(12218063707125898307)
XLA Ops:
  0.6 40.1 %shard_map.112 = f32[3,16,2,336]{3,2,1,0:T(2,128)S(1)} custom-call(f32[16,2,336]{2,1,0:T(2,128)} %r_ref.1, f32[3,16]{1,0:T(4,128)} %pos_ref.1, f32[1,16]{1,0:T(1,128)} %bitcast.9, f32[1,16]{1,0:T(1,128)} %bitcast.10, s32[1,16]{1,0:T(1,128)} %bitcast.11, s32[16,512]{1,0:T(8,128)} %flags_ref.1, f32[1,384]{1,0:T(1,128)} %constant.2.clone.orders_ref, ...), custom_call_target="tpu_custom_call" | custom-call | tf_op jit(solution)/shard_map/pallas_call | solution.py:573
  40.7 0.7 %slice_bitcast_fusion = (f32[16,2,336]{2,1,0:T(2,128)}, f32[16,2,336]{2,1,0:T(2,128)}, f32[16,2,336]{2,1,0:T(2,128)}) fusion(f32[3,16,2,336]{3,2,1,0:T(2,128)S(1)} %shard_map.112), kind=kLoop, calls=%fused_computation | loop fusion | bytes 258048 | tf_op jit(solution)/shard_map/squeeze | solution.py:635

commit v2 on v1

--- a/solution.py
+++ b/solution.py
@@ -28,7 +28,7 @@
 )
 ORDERS = (
     (1, 2, 4, 3, 12, 8, 6, 5, 7, 14, 10, 13, 9, 11, 15),
-    (0, 5, 6, 8, 7, 2, 10, 12, 1, 9, 14, 11, 13, 15, 3),
+    (0, 5, 6, 8, 7, 2, 10, 12, 9, 1, 14, 11, 13, 15, 3),
 )
 
 
@@ -92,7 +92,7 @@
     n, S, C, CP, terms,
     r_ref, pos_ref, rad_ref, az_ref, counts_ref, flags_ref, orders_ref, tilt_ref, axial_ref,
     out_ref,
-    r_v, t_raw, flags_v, rows_own, rows_oth, r_own, r_oth,
+    r_v, t_raw, pos_v, rad_v, az_v, counts_v, orders_v, flags_v, rows_own, rows_oth, r_own, r_oth,
     own1, own2, buf1, buf2, f_hi, f_lo, w_all, acc,
     t_hi, t_lo, tt_hi, tt_lo, gg_hi, gg_lo, g_raw, g_hi, g_lo,
     p_scr, q_scr, p_fin, q_fin, part_own, part_oth, s3, t3, p3, sums,
@@ -169,14 +169,25 @@
     t_copy = pltpu.make_async_copy(tilt_ref, t_raw, in_sem.at[1])
     f_copy = pltpu.make_async_copy(flags_ref, flags_v.at[core_rows, :], in_sem.at[2])
     g_copy = pltpu.make_async_copy(axial_ref, g_raw, in_sem.at[3])
-    for copy in (r_copy, t_copy, f_copy, g_copy):
+    small = [
+        pltpu.make_async_copy(ref, dst, in_sem.at[4 + i])
+        for i, (ref, dst) in enumerate(
+            (
+                (pos_ref, pos_v), (rad_ref, rad_v), (az_ref, az_v),
+                (counts_ref, counts_v), (orders_ref, orders_v),
+            )
+        )
+    ]
+    for copy in small + [r_copy, t_copy, f_copy, g_copy]:
         copy.start()
 
     rows_own[...] = jnp.zeros_like(rows_own)
-    rows_own[0:3, 0:S] = pos_ref[...]
-    rows_own[3:4, 0:S] = rad_ref[...]
-    rows_own[4:5, 0:S] = az_ref[...]
-    rows_own[5:6, 0:S] = counts_ref[...].astype(F32)
+    for copy in small:
+        copy.wait()
+    rows_own[0:3, 0:S] = pos_v[...]
+    rows_own[3:4, 0:S] = rad_v[...]
+    rows_own[4:5, 0:S] = az_v[...]
+    rows_own[5:6, 0:S] = counts_v[...].astype(F32)
     cols = rows_own[...].T[0:S]
     lane = lax.broadcasted_iota(jnp.int32, (S, CP), 1)
     lane2 = lax.broadcasted_iota(jnp.int32, (S2, CP), 1)
@@ -189,7 +200,7 @@
     def padded(v):
         return jnp.concatenate([v, jnp.zeros((v.shape[0], CP - C), v.dtype)], axis=1)
 
-    phases = cols[:, 4:5] * orders_ref[...]
+    phases = cols[:, 4:5] * orders_v[...]
     cos_o = jnp.cos(phases)
     sin_o = jnp.sin(phases)
     cos2 = jnp.concatenate([cos_o, cos_o], axis=0)
@@ -320,8 +331,11 @@
         return total
 
     def gather(phase, buf, fillers, on_plane):
-        fillers = list(fillers)
         steps = len(kinds[0][1])
+        relays = [
+            max([i for i, (_, nexts) in enumerate(takes) if nexts]) for _, takes in kinds
+        ]
+        calm = min(max(relays), steps - 1)
         gathered = None
         for i in range(steps):
             origin = pick([chip_at(own_bases, takes[i][0]) for _, takes in kinds])
@@ -343,13 +357,11 @@
                     ],
                 )
             absorb(buf, origin, slot)
-            if fillers:
-                fillers.pop(0)()
+            if i == calm:
+                for fill in fillers:
+                    fill()
             for s in range(q):
-                if ready[s] == i:
-                    if s == 0:
-                        while fillers:
-                            fillers.pop(0)()
+                if max(ready[s], calm) == i:
                     on_plane(s)
                     if s % 2 == 1:
                         gathered = gather_product(s // 2)
@@ -386,14 +398,13 @@
             ref[m * CP + C : (m + 1) * CP, :] = zeros_pad
 
     fill_tilt()
-    g_copy.wait()
     pair_wait(1, rows_oth)
     cols_oth = rows_oth[...].T[0:S]
     first = core == 0
     cols2 = jnp.concatenate(
         [jnp.where(first, cols, cols_oth), jnp.where(first, cols_oth, cols)], axis=0
     )
-    phases = cols2[:, 4:5] * orders_ref[...]
+    phases = cols2[:, 4:5] * orders_v[...]
     cos_t = jnp.cos(phases)
     sin_t = jnp.sin(phases)
     root = 1.0 / jnp.sqrt(1.0 + cols2[:, 5:6])
@@ -444,7 +455,11 @@
         v = dot3(high, low, tt_hi[...], tt_lo[...]) * root
         return cos_t * v - sin_t * swapped(v)
 
-    fillers = [functools.partial(fill_axial, m) for m in range(terms)] + [fill_gram]
+    early = terms - 2
+    g_copy.wait()
+    for m in range(early):
+        fill_axial(m)
+    fillers = [functools.partial(fill_axial, m) for m in range(early, terms)] + [fill_gram]
     coupled = couple(gather(0, buf1, fillers, weights))
 
     framed = buf1[chip_rows(chip), :]
@@ -496,14 +511,20 @@
         row = jnp.where(lane1 == i, total(a, b), row)
     sums[me] = row
 
-    def sum_copy(k, origin, dev):
-        return remote(
-            sums.at[origin], sums.at[origin], sum_send.at[k], sum_recv.at[origin], dev
-        )
-
-    @pl.loop(1, n)
-    def _(k):
-        sum_copy(k, me, lax.rem(me + k, n)).start()
+    def sum_copy(rows, dev):
+        return remote(sums.at[rows], sums.at[rows], sum_send, sum_recv, dev)
+
+    def sum_start(k):
+        away = k // 8
+        dev = 8 * lax.rem(z_at + away, q) + lax.rem(me + k, 8)
+        sum_copy(pl.ds(me, 1), dev).start()
+
+    far = sorted(range(1, n), key=lambda k: (-min(k // 8, q - k // 8), k))
+    if n <= 64:
+        for k in far:
+            sum_start(k)
+    else:
+        pl.loop(1, n)(sum_start)
 
     pair_wait(4, p_fin.at[1 - core])
     pair_wait(6, q_fin.at[1 - core])
@@ -523,11 +544,9 @@
 
         guarded(kind, body)
 
-    @pl.loop(1, n)
-    def _(k):
-        peer = lax.rem(me + k, n)
-        sum_copy(k, peer, peer).wait_recv()
-
+    everyone = sum_copy(pl.ds(0, n - 1), other)
+    everyone.wait_recv()
+    everyone.wait_send()
     all_sums = jnp.sum(sums[...], axis=0)
     t_s, t_t, r_s, r_t = [all_sums[:, i : i + 1] for i in range(4)]
     omega = t_s / t_t
@@ -542,10 +561,6 @@
     out_ref[0] = alpha * r_val + omega * s_val
     out_ref[1] = res
     out_ref[2] = res + beta * (r_val - omega * p3[...])
-
-    @pl.loop(1, n)
-    def _(k):
-        sum_copy(k, me, lax.rem(me + k, n)).wait_send()
 
 
 def solution(mesh):
@@ -573,11 +588,16 @@
         stacked = pl.pallas_call(
             functools.partial(kernel, n, S, C, CP, terms),
             out_shape=out,
-            in_specs=[anywhere, vmem, vmem, vmem, vmem, anywhere, vmem, anywhere, anywhere],
+            in_specs=[anywhere] * 9,
             out_specs=vmem,
             scratch_shapes=[
                 pltpu.VMEM((S, 2, C), F32),
                 pltpu.VMEM((C, C), F32),
+                pltpu.VMEM(positions.shape, F32),
+                pltpu.VMEM((1, S), F32),
+                pltpu.VMEM((1, S), F32),
+                pltpu.VMEM((1, S), jnp.int32),
+                pltpu.VMEM((1, CP), F32),
                 pltpu.VMEM((2 * S, total), jnp.int32),
                 pltpu.VMEM((8, LANES), F32),
                 pltpu.VMEM((8, LANES), F32),
@@ -610,13 +630,13 @@
                 pltpu.VMEM((S, 2, C), F32),
                 pltpu.VMEM((S, 2, C), F32),
                 pltpu.VMEM((n, 1, LANES), F32),
-                pltpu.SemaphoreType.DMA((4,)),
+                pltpu.SemaphoreType.DMA((9,)),
                 pltpu.SemaphoreType.DMA((2, most)),
                 pltpu.SemaphoreType.DMA((2, n // 2)),
                 pltpu.SemaphoreType.DMA((7,)),
                 pltpu.SemaphoreType.DMA((7,)),
-                pltpu.SemaphoreType.DMA((n,)),
-                pltpu.SemaphoreType.DMA((n,)),
+                pltpu.SemaphoreType.DMA,
+                pltpu.SemaphoreType.DMA,
             ],
             compiler_params=pltpu.CompilerParams(
                 collective_id=0, has_side_effects=True, vmem_limit_bytes=60 * 1024 * 1024

time: 41.5 us -> 39.8 us (0.959)
  Pallas kernels: 40.1 us -> 38.4 us
    pallas_call x1, Pallas kernels: 40.1 us -> 38.4 us  [on_device(): pl.pallas_call(functools.partial(kernel, n, S, C, CP, terms), out_shape=o...]
where the time goes in v2:
time: 39.8 us; the launch traced here: 39.7 us
  Pallas kernels  38.4 us (96%)
  local copies, waits for them, and re-layouts  0.67 us (2%)
  between operations  0.64 us (2%)
    pallas_call x1, Pallas kernels, on_device(): pl.pallas_call(functools.partial(kernel, n, S, C, CP, terms), out_shape=o...  38.4 us

profile of v2, /device:TPU:0, one launch (start us, length us, event | category | flops | bytes accessed | tf_op | source)
XLA Modules:
  0.0 39.7 jit_solution(17819509994234656229)
XLA Ops:
  0.6 38.4 %shard_map.112 = f32[3,16,2,336]{3,2,1,0:T(2,128)S(1)} custom-call(f32[16,2,336]{2,1,0:T(2,128)} %r_ref.1, f32[3,16]{1,0:T(4,128)} %pos_ref.1, f32[1,16]{1,0:T(1,128)} %bitcast.9, f32[1,16]{1,0:T(1,128)} %bitcast.10, s32[1,16]{1,0:T(1,128)} %bitcast.11, s32[16,512]{1,0:T(8,128)} %flags_ref.1, f32[1,384]{1,0:T(1,128)} %constant.2.clone.orders_ref, ...), custom_call_target="tpu_custom_call" | custom-call | tf_op jit(solution)/shard_map/pallas_call | solution.py:588
  39.0 0.7 %slice_bitcast_fusion = (f32[16,2,336]{2,1,0:T(2,128)}, f32[16,2,336]{2,1,0:T(2,128)}, f32[16,2,336]{2,1,0:T(2,128)}) fusion(f32[3,16,2,336]{3,2,1,0:T(2,128)S(1)} %shard_map.112), kind=kLoop, calls=%fused_computation | loop fusion | bytes 258048 | tf_op jit(solution)/shard_map/squeeze | solution.py:655
